TPU v7x, 128 devices: a whole 4x4x4 slice. The times are simulated.
128 devices in a mesh: lat: 8 (over x, core), lon: 16 (over z, y).
Axes of the slice: x: 4, y: 4, z: 4, core: 2. Of those that a mesh axis runs over, the one named last changes fastest.
Arguments:
- queries: bfloat16 [32768, 2048], P(('lat', 'lon')), may hold values from -340 to 340
- keys: bfloat16 [32768, 2048], P(('lat', 'lon')), may hold values from -12 to 12
- values: bfloat16 [32768, 2048], P(('lat', 'lon')), may hold values from -6 to 6
- partners: int32 [128, 13], P(('lat', 'lon')), may hold values from -1 to 127, as said below
- out_weight: bfloat16 [2048, 2048], P(None, 'lat'), may hold values from -0.125 to 0.125
Outputs:
- projected: bfloat16 [32768, 2048], P(('lat', 'lon'))
Inputs may be any that keep to these rules, and one draw needn't show every extreme that they name: `partners`: for each block, the first entries of its row are distinct blocks of its own band, none in its own sector or the two sectors beside it; the remaining entries are -1. In every band some block uses all 13 slots.
All inputs are finite; a program needn't handle non-finite values.
Results may differ from a plain program's by a relative error of at most 0.0095.
Values may be sent and summed in bfloat16 or wider, within the bound.
A program may use at most 128 MiB of HBM per device.

v0:
```python
import math

import jax
import jax.numpy as jnp
from jax import lax
from jax.sharding import PartitionSpec as P

HEADS = 16
HEAD_DIM = 128


very_low = -1e30


def in_one_piece(arrays, axis, dim, along):
    both = jnp.concatenate(arrays, axis=along)
    result, at, finished = (lax.all_gather(both, axis, axis=dim, tiled=True), 0, [])
    for a in arrays:
        finished.append(lax.slice_in_dim(result, at, at + a.shape[along], axis=along))
        at += a.shape[along]
    return tuple(finished)


def membership(listed_row, sector, band_start, sectors, lon_count):
    nearby = (
        (sectors == sector)
        | (sectors == (sector + 1) % lon_count)
        | (sectors == (sector + lon_count - 1) % lon_count)
    )
    named = jnp.any(listed_row[:, None] - band_start == sectors[None, :], axis=0)
    return nearby | named


def attend(running, query_block, key_block, value_block, score_scale):
    row_peak, row_total, mixture = running
    scores = (
        jnp.einsum("qhd,khd->hqk", query_block, key_block, preferred_element_type=jnp.float32)
        * score_scale
    )
    new_peak = jnp.maximum(row_peak, jnp.max(scores, axis=-1))
    shrink = jnp.exp(row_peak - new_peak)
    weights = jnp.exp(scores - new_peak[:, :, None])
    row_total = row_total * shrink + jnp.sum(weights, axis=-1)
    mixture = mixture * shrink.T[:, :, None] + jnp.einsum(
        "hqk,khd->qhd",
        weights.astype(jnp.bfloat16),
        value_block,
        preferred_element_type=jnp.float32,
    )
    return (new_peak, row_total, mixture)


def per_device(queries, keys, values, partners, out_weight):
    lon_count = lax.axis_size("lon")
    sector = lax.axis_index("lon")
    band_start = lax.axis_index("lat") * lon_count
    score_scale = 1.0 / math.sqrt(HEAD_DIM)
    sectors = jnp.arange(lon_count, dtype=jnp.int32)
    block_rows = queries.shape[0]
    member = membership(partners[0], sector, band_start, sectors, lon_count)
    query_block = queries.reshape(block_rows, HEADS, HEAD_DIM)
    initial = (
        jnp.full((HEADS, block_rows), very_low, jnp.float32),
        jnp.zeros((HEADS, block_rows), jnp.float32),
        jnp.zeros((block_rows, HEADS, HEAD_DIM), jnp.float32),
    )
    running = initial
    key_piece, value_piece = in_one_piece((keys, values), "lon", 0, 1)
    block_count = key_piece.shape[0] // block_rows
    key_blocks = key_piece.reshape(block_count, block_rows, HEADS, HEAD_DIM)
    value_blocks = value_piece.reshape(block_count, block_rows, HEADS, HEAD_DIM)

    def visit(held, element):
        key_block, value_block, offset = element
        listed = lax.dynamic_index_in_dim(member, offset, 0, keepdims=False)
        held = lax.cond(
            listed,
            lambda inner: attend(inner, query_block, key_block, value_block, score_scale),
            lambda inner: inner,
            held,
        )
        return (held, None)

    running, _ = lax.scan(
        visit, running, (key_blocks, value_blocks, jnp.arange(block_count, dtype=jnp.int32))
    )
    row_peak, row_total, mixture = running
    attended = (
        (mixture / row_total.T[:, :, None])
        .reshape(block_rows, HEADS * HEAD_DIM)
        .astype(jnp.bfloat16)
    )
    projected = jnp.dot(
        attended,
        lax.all_gather(out_weight, "lat", axis=1, tiled=True),
        preferred_element_type=jnp.float32,
    )
    return projected.astype(jnp.bfloat16)


def solution(mesh):
    return jax.shard_map(
        per_device,
        mesh=mesh,
        in_specs=(
            P(("lat", "lon"), None),
            P(("lat", "lon"), None),
            P(("lat", "lon"), None),
            P(("lat", "lon"), None),
            P(None, "lat"),
        ),
        out_specs=P(("lat", "lon"), None),
        check_vma=False,
    )
```

profile of v0, /device:TPU:105, one launch (start us, length us, event | category | flops | bytes accessed | tf_op | source)
XLA Modules:
  0.0 417.4 jit_solution(11262633813400237595)
XLA Ops:
  11.9 194.7 %all-gather.3.cloned.1.call-done = bf16[4096,4096]{1,0:T(8,128)(2,1)} async-done(((bf16[256,4096]{1,0:T(8,128)(2,1)}), bf16[4096,4096]{1,0:T(8,128)(2,1)}) %all-gather.3.cloned.1.call-update) | async-done | bytes 33554448 | tf_op jit(solution)/shard_map/all_gather | solution.py:17
  206.6 19.0 %slice_bitcast_fusion = (bf16[512,8,16,128]{3,1,2,0:T(8,128)(2,1)S(1)}, bf16[512,8,16,128]{3,1,2,0:T(8,128)(2,1)}) fusion(bf16[4096,4096]{1,0:T(8,128)(2,1)} %all-gather.3.cloned.1.call-done), kind=kLoop, calls=%fused_computation.20 | loop fusion | bytes 67108864
  225.6 9.7 %copy.20 = bf16[512,8,16,128]{3,2,1,0:T(8,128)(2,1)S(1)} copy(bf16[512,8,16,128]{3,1,2,0:T(8,128)(2,1)} %get-tuple-element.165) | data formatting | bytes 33554432
  235.3 8.1 %copy.15 = bf16[16,256,16,128]{3,1,2,0:T(8,128)(2,1)} copy(bf16[16,256,16,128]{3,2,1,0:T(8,128)(2,1)S(1)} %bitcast.46) | data formatting | bytes 33554432 | tf_op jit(solution)/shard_map/while | solution.py:84
  243.3 3.5 copy.21
  246.8 8.0 %copy.17 = bf16[16,256,16,128]{3,1,2,0:T(8,128)(2,1)} copy(bf16[16,256,16,128]{3,2,1,0:T(8,128)(2,1)S(1)} %bitcast.47) | data formatting | bytes 33554432 | tf_op jit(solution)/shard_map/while | solution.py:84
  255.1 145.1 %while.14 = (s32[]{:T(128)}, f32[16,256]{1,0:T(8,128)S(1)}, f32[16,256]{1,0:T(8,128)S(1)}, f32[256,16,128]{2,0,1:T(8,128)S(1)}, s32[16]{0:T(128)S(1)}, /*index=5...) while((s32[]{:T(128)}, f32[16,256]{1,0:T(8,128)S(1)}, ...), condition=%wide.region_6.7_spmd, body=%wide.region_1.6_spmd.sunk | while | flops 546320384 | bytes 20186396 | solution.py:84
  258.7 5.4 %conditional.2 = ((f32[16,256]{1,0:T(8,128)S(1)}, f32[16,256]{1,0:T(8,128)S(1)}, f32[256,16,128]{2,0,1:T(8,128)S(1)})) conditional(s32[]{:T(128)} %bitcast.45, (f32[16,256]{1,0:T(8,128)S(1)}, f32[16,256]{1,0:T(8,128)S(1)}, f32[256,16,128]{2,0,1:T(8,128)S(1)}) %tuple.36, (bf16[16,256,16,128]{3,1,2,0:T(8,128)(2,1)}, s32[]{:T(128)}, ...), branch_computations={%region_2.2_spmd, %region_3.5_spmd} | conditional | flops 546320384 | bytes 20186144 | solution.py:76
  267.8 5.4 %conditional.2 = ((f32[16,256]{1,0:T(8,128)S(1)}, f32[16,256]{1,0:T(8,128)S(1)}, f32[256,16,128]{2,0,1:T(8,128)S(1)})) conditional(s32[]{:T(128)} %bitcast.45, (f32[16,256]{1,0:T(8,128)S(1)}, f32[16,256]{1,0:T(8,128)S(1)}, f32[256,16,128]{2,0,1:T(8,128)S(1)}) %tuple.36, (bf16[16,256,16,128]{3,1,2,0:T(8,128)(2,1)}, s32[]{:T(128)}, ...), branch_computations={%region_2.2_spmd, %region_3.5_spmd} | conditional | flops 546320384 | bytes 20186144 | solution.py:76
  276.9 5.4 %conditional.2 = ((f32[16,256]{1,0:T(8,128)S(1)}, f32[16,256]{1,0:T(8,128)S(1)}, f32[256,16,128]{2,0,1:T(8,128)S(1)})) conditional(s32[]{:T(128)} %bitcast.45, (f32[16,256]{1,0:T(8,128)S(1)}, f32[16,256]{1,0:T(8,128)S(1)}, f32[256,16,128]{2,0,1:T(8,128)S(1)}) %tuple.36, (bf16[16,256,16,128]{3,1,2,0:T(8,128)(2,1)}, s32[]{:T(128)}, ...), branch_computations={%region_2.2_spmd, %region_3.5_spmd} | conditional | flops 546320384 | bytes 20186144 | solution.py:76
  286.0 5.4 %conditional.2 = ((f32[16,256]{1,0:T(8,128)S(1)}, f32[16,256]{1,0:T(8,128)S(1)}, f32[256,16,128]{2,0,1:T(8,128)S(1)})) conditional(s32[]{:T(128)} %bitcast.45, (f32[16,256]{1,0:T(8,128)S(1)}, f32[16,256]{1,0:T(8,128)S(1)}, f32[256,16,128]{2,0,1:T(8,128)S(1)}) %tuple.36, (bf16[16,256,16,128]{3,1,2,0:T(8,128)(2,1)}, s32[]{:T(128)}, ...), branch_computations={%region_2.2_spmd, %region_3.5_spmd} | conditional | flops 546320384 | bytes 20186144 | solution.py:76
  295.0 5.4 %conditional.2 = ((f32[16,256]{1,0:T(8,128)S(1)}, f32[16,256]{1,0:T(8,128)S(1)}, f32[256,16,128]{2,0,1:T(8,128)S(1)})) conditional(s32[]{:T(128)} %bitcast.45, (f32[16,256]{1,0:T(8,128)S(1)}, f32[16,256]{1,0:T(8,128)S(1)}, f32[256,16,128]{2,0,1:T(8,128)S(1)}) %tuple.36, (bf16[16,256,16,128]{3,1,2,0:T(8,128)(2,1)}, s32[]{:T(128)}, ...), branch_computations={%region_2.2_spmd, %region_3.5_spmd} | conditional | flops 546320384 | bytes 20186144 | solution.py:76
  304.1 5.4 %conditional.2 = ((f32[16,256]{1,0:T(8,128)S(1)}, f32[16,256]{1,0:T(8,128)S(1)}, f32[256,16,128]{2,0,1:T(8,128)S(1)})) conditional(s32[]{:T(128)} %bitcast.45, (f32[16,256]{1,0:T(8,128)S(1)}, f32[16,256]{1,0:T(8,128)S(1)}, f32[256,16,128]{2,0,1:T(8,128)S(1)}) %tuple.36, (bf16[16,256,16,128]{3,1,2,0:T(8,128)(2,1)}, s32[]{:T(128)}, ...), branch_computations={%region_2.2_spmd, %region_3.5_spmd} | conditional | flops 546320384 | bytes 20186144 | solution.py:76
  313.2 5.4 %conditional.2 = ((f32[16,256]{1,0:T(8,128)S(1)}, f32[16,256]{1,0:T(8,128)S(1)}, f32[256,16,128]{2,0,1:T(8,128)S(1)})) conditional(s32[]{:T(128)} %bitcast.45, (f32[16,256]{1,0:T(8,128)S(1)}, f32[16,256]{1,0:T(8,128)S(1)}, f32[256,16,128]{2,0,1:T(8,128)S(1)}) %tuple.36, (bf16[16,256,16,128]{3,1,2,0:T(8,128)(2,1)}, s32[]{:T(128)}, ...), branch_computations={%region_2.2_spmd, %region_3.5_spmd} | conditional | flops 546320384 | bytes 20186144 | solution.py:76
  322.2 5.4 %conditional.2 = ((f32[16,256]{1,0:T(8,128)S(1)}, f32[16,256]{1,0:T(8,128)S(1)}, f32[256,16,128]{2,0,1:T(8,128)S(1)})) conditional(s32[]{:T(128)} %bitcast.45, (f32[16,256]{1,0:T(8,128)S(1)}, f32[16,256]{1,0:T(8,128)S(1)}, f32[256,16,128]{2,0,1:T(8,128)S(1)}) %tuple.36, (bf16[16,256,16,128]{3,1,2,0:T(8,128)(2,1)}, s32[]{:T(128)}, ...), branch_computations={%region_2.2_spmd, %region_3.5_spmd} | conditional | flops 546320384 | bytes 20186144 | solution.py:76
  331.3 5.4 %conditional.2 = ((f32[16,256]{1,0:T(8,128)S(1)}, f32[16,256]{1,0:T(8,128)S(1)}, f32[256,16,128]{2,0,1:T(8,128)S(1)})) conditional(s32[]{:T(128)} %bitcast.45, (f32[16,256]{1,0:T(8,128)S(1)}, f32[16,256]{1,0:T(8,128)S(1)}, f32[256,16,128]{2,0,1:T(8,128)S(1)}) %tuple.36, (bf16[16,256,16,128]{3,1,2,0:T(8,128)(2,1)}, s32[]{:T(128)}, ...), branch_computations={%region_2.2_spmd, %region_3.5_spmd} | conditional | flops 546320384 | bytes 20186144 | solution.py:76
  340.4 5.4 %conditional.2 = ((f32[16,256]{1,0:T(8,128)S(1)}, f32[16,256]{1,0:T(8,128)S(1)}, f32[256,16,128]{2,0,1:T(8,128)S(1)})) conditional(s32[]{:T(128)} %bitcast.45, (f32[16,256]{1,0:T(8,128)S(1)}, f32[16,256]{1,0:T(8,128)S(1)}, f32[256,16,128]{2,0,1:T(8,128)S(1)}) %tuple.36, (bf16[16,256,16,128]{3,1,2,0:T(8,128)(2,1)}, s32[]{:T(128)}, ...), branch_computations={%region_2.2_spmd, %region_3.5_spmd} | conditional | flops 546320384 | bytes 20186144 | solution.py:76
  349.5 5.4 %conditional.2 = ((f32[16,256]{1,0:T(8,128)S(1)}, f32[16,256]{1,0:T(8,128)S(1)}, f32[256,16,128]{2,0,1:T(8,128)S(1)})) conditional(s32[]{:T(128)} %bitcast.45, (f32[16,256]{1,0:T(8,128)S(1)}, f32[16,256]{1,0:T(8,128)S(1)}, f32[256,16,128]{2,0,1:T(8,128)S(1)}) %tuple.36, (bf16[16,256,16,128]{3,1,2,0:T(8,128)(2,1)}, s32[]{:T(128)}, ...), branch_computations={%region_2.2_spmd, %region_3.5_spmd} | conditional | flops 546320384 | bytes 20186144 | solution.py:76
  358.5 5.4 %conditional.2 = ((f32[16,256]{1,0:T(8,128)S(1)}, f32[16,256]{1,0:T(8,128)S(1)}, f32[256,16,128]{2,0,1:T(8,128)S(1)})) conditional(s32[]{:T(128)} %bitcast.45, (f32[16,256]{1,0:T(8,128)S(1)}, f32[16,256]{1,0:T(8,128)S(1)}, f32[256,16,128]{2,0,1:T(8,128)S(1)}) %tuple.36, (bf16[16,256,16,128]{3,1,2,0:T(8,128)(2,1)}, s32[]{:T(128)}, ...), branch_computations={%region_2.2_spmd, %region_3.5_spmd} | conditional | flops 546320384 | bytes 20186144 | solution.py:76
  367.6 5.4 %conditional.2 = ((f32[16,256]{1,0:T(8,128)S(1)}, f32[16,256]{1,0:T(8,128)S(1)}, f32[256,16,128]{2,0,1:T(8,128)S(1)})) conditional(s32[]{:T(128)} %bitcast.45, (f32[16,256]{1,0:T(8,128)S(1)}, f32[16,256]{1,0:T(8,128)S(1)}, f32[256,16,128]{2,0,1:T(8,128)S(1)}) %tuple.36, (bf16[16,256,16,128]{3,1,2,0:T(8,128)(2,1)}, s32[]{:T(128)}, ...), branch_computations={%region_2.2_spmd, %region_3.5_spmd} | conditional | flops 546320384 | bytes 20186144 | solution.py:76
  376.7 5.4 %conditional.2 = ((f32[16,256]{1,0:T(8,128)S(1)}, f32[16,256]{1,0:T(8,128)S(1)}, f32[256,16,128]{2,0,1:T(8,128)S(1)})) conditional(s32[]{:T(128)} %bitcast.45, (f32[16,256]{1,0:T(8,128)S(1)}, f32[16,256]{1,0:T(8,128)S(1)}, f32[256,16,128]{2,0,1:T(8,128)S(1)}) %tuple.36, (bf16[16,256,16,128]{3,1,2,0:T(8,128)(2,1)}, s32[]{:T(128)}, ...), branch_computations={%region_2.2_spmd, %region_3.5_spmd} | conditional | flops 546320384 | bytes 20186144 | solution.py:76
  385.7 5.4 %conditional.2 = ((f32[16,256]{1,0:T(8,128)S(1)}, f32[16,256]{1,0:T(8,128)S(1)}, f32[256,16,128]{2,0,1:T(8,128)S(1)})) conditional(s32[]{:T(128)} %bitcast.45, (f32[16,256]{1,0:T(8,128)S(1)}, f32[16,256]{1,0:T(8,128)S(1)}, f32[256,16,128]{2,0,1:T(8,128)S(1)}) %tuple.36, (bf16[16,256,16,128]{3,1,2,0:T(8,128)(2,1)}, s32[]{:T(128)}, ...), branch_computations={%region_2.2_spmd, %region_3.5_spmd} | conditional | flops 546320384 | bytes 20186144 | solution.py:76
  394.8 5.4 %conditional.2 = ((f32[16,256]{1,0:T(8,128)S(1)}, f32[16,256]{1,0:T(8,128)S(1)}, f32[256,16,128]{2,0,1:T(8,128)S(1)})) conditional(s32[]{:T(128)} %bitcast.45, (f32[16,256]{1,0:T(8,128)S(1)}, f32[16,256]{1,0:T(8,128)S(1)}, f32[256,16,128]{2,0,1:T(8,128)S(1)}) %tuple.36, (bf16[16,256,16,128]{3,1,2,0:T(8,128)(2,1)}, s32[]{:T(128)}, ...), branch_computations={%region_2.2_spmd, %region_3.5_spmd} | conditional | flops 546320384 | bytes 20186144 | solution.py:76
  403.9 6.7 %convolution_convert_fusion = bf16[256,2048]{1,0:T(8,128)(2,1)} fusion(bf16[256,2048]{0,1:T(8,128)(2,1)S(1)} %bitcast.48, bf16[2048,2048]{1,0:T(8,128)(2,1)} %all-gather.5.cloned.1.call-done), kind=kOutput, calls=%fused_computation.22 | convolution fusion | flops 2148007936 | bytes 10485760 | tf_op jit(solution)/shard_map/dot_general | solution.py:93
  (149 shorter events, 113.4 us)
Async XLA Ops:
  6.5 4.0 copy-start
  6.5 200.1 %all-gather.3.cloned.1.call-start = ((), (), s32[]{:S(2)}) async-start(), calls=%async_computation | async-start | bytes 35651584 | tf_op jit(solution)/shard_map/all_gather | solution.py:17
  9.7 2.0 copy-start.1
  9.8 394.1 %all-gather.5.cloned.1.call-start = ((), (), s32[]{:S(2)}) async-start(), calls=%async_computation.1 | async-start | bytes 9437184 | tf_op jit(solution)/shard_map/all_gather | solution.py:95
Sparse Core Ops, SparseCore 0:
  9.9 196.6 all-gather.2
  208.3 55.0 all-gather.4
where the time goes:
time: 422 us; the launch traced here: 417 us
  waiting for transfers between devices  195 us (46%)
  matrix products  79.9 us (19%)
  local copies, waits for them, and re-layouts  70.6 us (17%)
  loops' own time  40.9 us (10%)
  other arithmetic  17 us (4%)
  between operations  13.5 us (3%)
    all_gather x1, waiting for transfers between devices, in_one_piece(): lax.all_gather(both, axis, axis=dim, tiled=True)  195 us
    dot_general x16, matrix products, attend(): jnp.einsum('hqk,khd->qhd', weights.astype(jnp.bfloat16), value_block, pre...  42.1 us
    another operation x1, loops' own time, per_device(): lax.scan(visit, running, (key_blocks, value_blocks, jnp.arange(block_coun...  40 us
    unnamed x8, local copies, waits for them, and re-layouts  32.6 us
    dot_general x16, matrix products, attend(): jnp.einsum('qhd,khd->hqk', query_block, key_block, preferred_element_type...  31.1 us
    while x4, local copies, waits for them, and re-layouts, per_device(): lax.scan(visit, running, (key_blocks, value_blocks, jnp.arange(block_coun...  18.7 us
    reduce_sum x16, other arithmetic, attend(): row_total = row_total * shrink + jnp.sum(weights, axis=-1)  11.5 us
    dynamic_slice x16, local copies, waits for them, and re-layouts, visit(): listed = lax.dynamic_index_in_dim(member, offset, 0, keepdims=False)  9.55 us
  transfers between devices with their start and end apart: 2, of which 1 were waited for; matrix products, arithmetic and copies ran while one was open for 38% of the time, Pallas kernels for 0%

commit v1 on v0

v1 whole, which is shorter than its diff:
```python
import math

import jax
import jax.numpy as jnp
from jax import lax
from jax.experimental import pallas as pl
from jax.experimental.pallas import tpu as pltpu
from jax.sharding import PartitionSpec as P

NB = 16
BLK = 256
HALF = BLK // 2
HD = 128
VR = 144
D = 2048
SCALE = math.log2(math.e) / math.sqrt(HD)
LOW = -1e30


def split_q(q):
    x = q.astype(jnp.float32) * SCALE
    high = x.astype(jnp.bfloat16)
    low = (x - high.astype(jnp.float32)).astype(jnp.bfloat16)
    return jnp.concatenate([high, low], axis=1)


def bias_of(row, block):
    j = lax.broadcasted_iota(jnp.int32, (NB, HALF), 0)
    named = jnp.max(jnp.where(row == j, 1.0, 0.0), axis=1, keepdims=True) > 0.5
    near = (j == block) | (j == lax.rem(block + 1, NB)) | (j == lax.rem(block + NB - 1, NB))
    return jnp.where(named | near, 0.0, LOW)


CHUNK = 2


def scores(qx, bias, k_ref, s_ref, sub_ref):
    best = None
    for c in range(0, NB, CHUNK):
        keys = k_ref[c:c + CHUNK].reshape(CHUNK * BLK, HD)
        s = lax.dot_general(
            jnp.concatenate([keys, keys], axis=1), qx, (((1,), (1,)), ((), ())),
            preferred_element_type=jnp.float32,
        )
        s_ref[c * BLK:(c + CHUNK) * BLK, :] = s
        for j in range(CHUNK):
            part = jnp.max(s[j * BLK:(j + 1) * BLK].reshape(BLK // 8, 8, BLK), axis=0)
            part = part + bias[c + j:c + j + 1, :]
            best = part if best is None else jnp.maximum(best, part)
    sub_ref[...] = jnp.max(best, axis=0, keepdims=True) - bias


def mix(s_ref, sub_ref, vt_ref):
    total = None
    for c in range(0, NB, CHUNK):
        w = [
            jnp.exp2(s_ref[j * BLK:(j + 1) * BLK, :] - sub_ref[j:j + 1, :]).astype(jnp.bfloat16)
            for j in range(c, c + CHUNK)
        ]
        part = jnp.dot(
            vt_ref[:, c * BLK:(c + CHUNK) * BLK], jnp.concatenate(w, axis=0),
            preferred_element_type=jnp.float32,
        )
        total = part if total is None else total + part
    return (total[0:HD] / total[HD:HD + 1]).astype(jnp.bfloat16)


MESH = pl.DeviceIdType.MESH
DIST = (1, 3, 2)
RING = [(0, 0, dz, dy) for dz in range(4) for dy in range(4) if dz or dy]
UNITS = [(0, 0), (1, 0), (3, 0), (2, 0), (0, 1), (0, 3), (0, 2)]
UNITS += [(1, 1), (1, 3), (3, 1), (3, 3), (2, 2), (1, 2), (2, 1), (3, 2), (2, 3)]
EARLY = 12


def wrap(a, d):
    return lax.rem(a + d, 4)


def back(d):
    return (4 - d) % 4


def ds128(i, n=1):
    return pl.ds(pl.multiple_of(i * 128, 128), n * 128)


class Place:
    def __init__(self):
        lat, lon = lax.axis_index("lat"), lax.axis_index("lon")
        self.x, self.core, self.z, self.y = lat // 2, lax.rem(lat, 2), lon // 4, lax.rem(lon, 4)
        self.lat, self.lon = lat, lon

    def at(self, dx, dc, dz, dy):
        return (
            wrap(self.x, dx) * 2 + lax.rem(self.core + dc, 2),
            wrap(self.z, dz) * 4 + wrap(self.y, dy),
        )

    def lon_at(self, dz, dy):
        return wrap(self.z, dz) * 4 + wrap(self.y, dy)


def remote(src, dst, ss, rs, to):
    return pltpu.make_async_remote_copy(
        src_ref=src, dst_ref=dst, send_sem=ss, recv_sem=rs, device_id=to, device_id_type=MESH
    )


def arrived(buf, sem):
    pltpu.make_async_copy(buf, buf, sem).wait()


def along(half, first, second):
    return (second, first) if half == 0 else (first, second)


class Exchange:
    def __init__(self, place, piece, landing, mid, s1, r1, s2, r2):
        self.place, self.piece, self.landing, self.mid = place, piece, landing, mid
        self.s1, self.r1, self.s2, self.r2 = s1, r1, s2, r2

    def start(self):
        place = self.place
        for d in DIST:
            for g in (0, 1, 3, 2):
                for half in range(2):
                    to = place.at(0, 0, *along(half, d, 0))
                    src = self.piece(half, place.lon_at(*along(half, d, g)))
                    dst = self.mid.at[half, d - 1, g - 1] if g else self.landing(half, d, 0, place.lon)
                    k = min(g, 1)
                    remote(src, dst, self.s1.at[half, d - 1, k], self.r1.at[half, d - 1, k], to).start()
        for g in DIST:
            for half in range(2):
                o = along(half, 0, g)
                remote(
                    self.piece(half, place.lon_at(*o)), self.landing(half, 0, g, place.lon),
                    self.s2.at[half, g - 1, 0], self.r2.at[half, g - 1, 0], place.at(0, 0, *o),
                ).start()

    def pass_on(self, d):
        place = self.place
        for half in range(2):
            arrived(self.mid.at[half, d - 1], self.r1.at[half, d - 1, 1])
            block = place.lon_at(*along(half, 4 - d, 0))
            for g in DIST:
                remote(
                    self.mid.at[half, d - 1, g - 1], self.landing(half, d, g, block),
                    self.s2.at[half, g - 1, d], self.r2.at[half, g - 1, d],
                    place.at(0, 0, *along(half, 0, g)),
                ).start()

    def landed(self, half, d, g):
        block = self.place.lon_at(*along(half, back(d), back(g)))
        ref = self.landing(half, d, g, block)
        if g:
            arrived(ref, self.r2.at[half, g - 1, d])
        elif d:
            arrived(ref, self.r1.at[half, d - 1, 0])
        return block, ref

    def sent(self):
        one = self.mid.at[0, 0, 0]
        for half in range(2):
            for d in range(3):
                arrived(one, self.s1.at[half, d, 0])
                arrived(self.mid.at[half, d], self.s1.at[half, d, 1])
                for g in range(4):
                    arrived(one, self.s2.at[half, d, g])


def kernel(
    q, k, v, w, p, out,
    mine, kland, vland, qland, table, vt, sa, sb, ba, bb, osend, heads, att, partial, weight, mid,
    ks1, kr1, ks2, kr2, vs1, vr1, vs2, vr2, qs1, qr1, qs2, qr2,
    os, orr, ws, wr, ps, pr, lsem,
):
    place = Place()
    lat, lon = place.lat, place.lon
    rows = (pl.ds(0, HALF), pl.ds(HALF, HALF))
    loads = [pltpu.make_async_copy(a, mine.at[n], lsem.at[n]) for n, a in enumerate((k, v, q))]
    for c in loads:
        c.start()
    local = [
        pltpu.make_async_copy(k.at[:, ds128(lon)], kland.at[lon], lsem.at[3]),
        pltpu.make_async_copy(v.at[:, ds128(lon)], vland.at[lon], lsem.at[4]),
        pltpu.make_async_copy(q.at[:, ds128(lon)], qland.at[0], lsem.at[5]),
        pltpu.make_async_copy(w, weight.at[lat], lsem.at[6]),
        pltpu.make_async_copy(p, table.at[lon], lsem.at[7]),
    ]
    for c in local:
        c.start()

    peers = RING + [(1, 0, 0, 0), (3, 0, 0, 0), (0, 1, 0, 0)]
    bar = pltpu.get_barrier_semaphore()
    for o in peers:
        pl.semaphore_signal(bar, inc=1, device_id=place.at(*o), device_id_type=MESH)
    pl.semaphore_wait(bar, len(peers))

    started = []

    def send(*args):
        c = remote(*args)
        c.start()
        started.append(c)

    for n, o in enumerate(RING):
        send(p, table.at[lon], ps.at[n], pr.at[n], place.at(*o))

    def exchange(n, landing, *sems):
        return Exchange(
            place, lambda half, head: mine.at[n, rows[half], ds128(head)], landing, mid.at[n], *sems
        )

    ke = exchange(0, lambda half, d, g, b: kland.at[b, rows[half]], ks1, kr1, ks2, kr2)
    ve = exchange(1, lambda half, d, g, b: vland.at[b, rows[half]], vs1, vr1, vs2, vr2)
    qe = exchange(2, lambda half, d, g, b: qland.at[UNITS.index((d, g)), rows[half]], qs1, qr1, qs2, qr2)
    loads[0].wait()
    ke.start()
    send(w, weight.at[lat], ws.at[0], wr.at[0], place.at(1, 0, 0, 0))
    send(w, weight.at[lat], ws.at[1], wr.at[1], place.at(3, 0, 0, 0))
    send(w, weight.at[lat], ws.at[2], wr.at[2], place.at(0, 1, 0, 0))
    loads[1].wait()
    ve.start()
    loads[2].wait()
    for d in DIST:
        ke.pass_on(d)
    for d in DIST:
        ve.pass_on(d)
    qe.start()

    for c in local:
        c.wait()
    for n in range(len(RING)):
        arrived(table.at[0], pr.at[n])
    vt[HD:VR, :] = jnp.where(
        lax.broadcasted_iota(jnp.int32, (VR - HD, NB * BLK), 0) == 0, 1.0, 0.0
    ).astype(jnp.bfloat16)

    def turn(half, d, g):
        b, ref = ve.landed(half, d, g)
        vt[0:HD, ds128(2 * b + half)] = ref[...].T

    for half in range(2):
        for d, g in UNITS[:7]:
            turn(half, d, g)
    for d, g in UNITS[1:]:
        for half in range(2):
            ke.landed(half, d, g)

    def unit_blocks(u):
        d, g = UNITS[u]
        return [place.lon_at(*along(half, back(d), back(g))) for half in range(2)]

    S, B = (sa, sb), (ba, bb)

    def score(u):
        bias = [bias_of(table[b][0:1, :], b) for b in unit_blocks(u)]
        scores(split_q(qland[u]), jnp.concatenate(bias, axis=1), kland, S[u % 2], B[u % 2])

    score(0)
    for d, g in UNITS[7:]:
        for half in range(2):
            turn(half, d, g)

    left, right, far = (wrap(place.x, n) * 2 + place.core for n in (3, 1, 2))
    top, low = pl.ds(0, D // 2), pl.ds(D // 2, D // 2)

    def ring(src, n, to):
        send(src, src, ws.at[n], wr.at[n], to)

    def weight_step(u):
        if u == 3:
            arrived(weight.at[left], wr.at[0])
            ring(weight.at[left, top], 3, place.at(1, 0, 0, 0))
            ring(weight.at[left], 4, place.at(0, 1, 0, 0))
            arrived(weight.at[right], wr.at[1])
            ring(weight.at[right, low], 5, place.at(3, 0, 0, 0))
            ring(weight.at[right], 6, place.at(0, 1, 0, 0))
        if u == 13:
            arrived(weight.at[far, top], wr.at[3])
            ring(weight.at[far, top], 7, place.at(0, 1, 0, 0))
            arrived(weight.at[far, low], wr.at[5])
            ring(weight.at[far, low], 8, place.at(0, 1, 0, 0))

    def give_back(u):
        d, g = UNITS[u]
        if u == 0:
            return
        for half in range(2):
            dz, dy = along(half, d, g)
            lanes = pl.ds(half * HALF, HALF)
            send(
                osend.at[u, :, lanes], heads.at[UNITS.index((dz, dy)), :, lanes],
                os.at[u, half], orr.at[u, half], place.at(0, 0, back(dz), back(dy)),
            )

    for u in range(NB):
        if u < NB - 1:
            d, g = UNITS[u + 1]
            if g == 0:
                qe.pass_on(d)
            for half in range(2):
                qe.landed(half, d, g)
            score(u + 1)
        if u == 0:
            heads[0] = mix(S[0], B[0], vt)
        else:
            osend[u] = mix(S[u % 2], B[u % 2], vt)
            give_back(u - 1)
        weight_step(u)

    for n in (2, 4, 6):
        arrived(weight.at[0], wr.at[n])
    for n in (7, 8):
        arrived(weight.at[0, top], wr.at[n])

    def fetch(units):
        for u in units:
            for half in range(2):
                if u:
                    arrived(osend.at[0, :, pl.ds(0, HALF)], orr.at[u, half])
        for u in units:
            att[:, u * HD:(u + 1) * HD] = heads[u].T

    def weight_rows(units, n):
        return jnp.concatenate(
            [weight[n, ds128(place.lon_at(*UNITS[u])), :] for u in units], axis=0
        )

    give_back(NB - 1)
    fetch(range(EARLY))

    def first(n, _):
        partial[n] = jnp.dot(
            att[:, 0:EARLY * HD], weight_rows(range(EARLY), n), preferred_element_type=jnp.float32
        )
        return 0

    lax.fori_loop(0, 8, first, 0)
    fetch(range(EARLY, NB))
    for n in range(8):
        out[:, n * 256:(n + 1) * 256] = (
            partial[n]
            + jnp.dot(
                att[:, EARLY * HD:], weight_rows(range(EARLY, NB), n), preferred_element_type=jnp.float32
            )
        ).astype(jnp.bfloat16)
    for e in (ke, ve, qe):
        e.sent()
    for c in started:
        c.wait_send()


def per_device(queries, keys, values, partners, out_weight):
    band_start = lax.axis_index("lat") * NB
    listed = jnp.where(partners >= 0, partners - band_start, -1)
    listed = jnp.pad(listed, ((0, 7), (0, 128 - listed.shape[1])), constant_values=-1)
    hbm, vmem = pl.BlockSpec(memory_space=pltpu.HBM), pl.BlockSpec(memory_space=pltpu.VMEM)
    dma = pltpu.SemaphoreType.DMA
    bf16, f32 = jnp.bfloat16, jnp.float32
    return pl.pallas_call(
        kernel,
        out_shape=jax.ShapeDtypeStruct((BLK, D), bf16),
        in_specs=[hbm] * 4 + [vmem],
        out_specs=vmem,
        scratch_shapes=[
            pltpu.VMEM((3, BLK, D), bf16),
            pltpu.VMEM((NB, BLK, HD), bf16),
            pltpu.VMEM((NB, BLK, HD), bf16),
            pltpu.VMEM((NB, BLK, HD), bf16),
            pltpu.VMEM((NB, 8, 128), jnp.int32),
            pltpu.VMEM((VR, NB * BLK), bf16),
            pltpu.VMEM((NB * BLK, BLK), f32),
            pltpu.VMEM((NB * BLK, BLK), f32),
            pltpu.VMEM((NB, BLK), f32),
            pltpu.VMEM((NB, BLK), f32),
            pltpu.VMEM((NB, HD, BLK), bf16),
            pltpu.VMEM((NB, HD, BLK), bf16),
            pltpu.VMEM((BLK, D), bf16),
            pltpu.VMEM((8, BLK, 256), f32),
            pltpu.VMEM((8, D, 256), bf16),
            pltpu.VMEM((3, 2, 3, 3, HALF, HD), bf16),
        ]
        + [dma((2, 3, 2)), dma((2, 3, 2)), dma((2, 3, 4)), dma((2, 3, 4))] * 3
        + [dma((NB, 2)), dma((NB, 2)), dma((9,)), dma((9,)), dma((15,)), dma((15,)), dma((8,))],
        name="band_attention",
        compiler_params=pltpu.CompilerParams(
            collective_id=0, has_side_effects=True, vmem_limit_bytes=60 * 1024 * 1024
        ),
    )(queries, keys, values, out_weight, listed)


def solution(mesh):
    return jax.shard_map(
        per_device,
        mesh=mesh,
        in_specs=(
            P(("lat", "lon"), None),
            P(("lat", "lon"), None),
            P(("lat", "lon"), None),
            P(("lat", "lon"), None),
            P(None, "lat"),
        ),
        out_specs=P(("lat", "lon"), None),
        check_vma=False,
    )
```

time: 422 us -> 77.9 us (0.18)
  the two profiles are of different devices: /device:TPU:105 before, /device:TPU:1 now
where the time goes in v1:
time: 77.9 us; the launch traced here: 77.4 us
  Pallas kernels  73.8 us (95%)
  local copies, waits for them, and re-layouts  3.56 us (5%)
    pallas_call x1, Pallas kernels, per_device(): pl.pallas_call(kernel, out_shape=jax.ShapeDtypeStruct((BLK, D), bf16), in...  73.8 us
    unnamed x3, local copies, waits for them, and re-layouts  2.96 us

profile of v1, /device:TPU:1, one launch (start us, length us, event | category | flops | bytes accessed | tf_op | source)
XLA Modules:
  0.0 77.4 jit_solution(14444920196661528109)
XLA Ops:
  0.0 0.0 copy-start
  0.0 0.7 copy-done
  0.7 0.6 pad.4.p
  1.3 73.8 %band_attention.1 = bf16[256,2048]{1,0:T(8,128)(2,1)} custom-call(bf16[256,2048]{1,0:T(8,128)(2,1)} %q.1, bf16[256,2048]{1,0:T(8,128)(2,1)} %k.1, bf16[256,2048]{1,0:T(8,128)(2,1)} %v.1, bf16[2048,256]{1,0:T(8,128)(2,1)} %w.1, s32[8,128]{1,0:T(8,128)} %pad.4.p), custom_call_target="tpu_custom_call" | custom-call | tf_op jit(solution)/shard_map/band_attention/pallas_call | solution.py:362
  75.1 2.3 %copy.7 = bf16[256,2048]{1,0:T(8,128)(2,1)} copy(bf16[256,2048]{1,0:T(8,128)(2,1)} %band_attention.1) | data formatting | bytes 2097152
  (1 shorter events, 0.0 us)
Async XLA Ops:
  0.0 0.7 copy-start

commit v2 on v1

v2 whole, which is shorter than its diff:
```python
import math

import jax
import jax.numpy as jnp
from jax import lax
from jax.experimental import pallas as pl
from jax.experimental.pallas import tpu as pltpu
from jax.sharding import PartitionSpec as P

NB = 16
BLK = 256
HALF = BLK // 2
HD = 128
VR = 144
D = 2048
SCALE = math.log2(math.e) / math.sqrt(HD)
LOW = -1e30
SLOTS = 13


def split_q(q):
    x = q.astype(jnp.float32) * SCALE
    high = x.astype(jnp.bfloat16)
    low = (x - high.astype(jnp.float32)).astype(jnp.bfloat16)
    return jnp.concatenate([high, low], axis=1)


def bias_of(row, block, band_start):
    j = lax.broadcasted_iota(jnp.int32, (NB, SLOTS), 0)
    named = jnp.max(jnp.where(row == j + band_start, 1.0, 0.0), axis=1, keepdims=True)
    j = lax.broadcasted_iota(jnp.int32, (NB, BLK), 0)
    near = (j == block) | (j == lax.rem(block + 1, NB)) | (j == lax.rem(block + NB - 1, NB))
    return jnp.where(near, 0.0, jnp.where(named > 0.5, 0.0, LOW))


def step(s_ref, w_ref, sub_ref, vt_ref, k_ref, qx=None, bias=None, weigh=True, blend=True):
    best, total = None, None
    for j in range(NB):
        at = slice(j * BLK, (j + 1) * BLK)
        if blend:
            part = jnp.dot(vt_ref[:, at], w_ref[at, :], preferred_element_type=jnp.float32)
            total = part if total is None else total + part
        if weigh:
            less = sub_ref[j:j + 1, :]
            for r in range(j * BLK, (j + 1) * BLK, 16):
                w_ref[r:r + 16, :] = jnp.exp2(s_ref[r:r + 16, :] - less).astype(jnp.bfloat16)
        if qx is not None:
            keys = k_ref[j]
            s = lax.dot_general(
                jnp.concatenate([keys, keys], axis=1), qx, (((1,), (1,)), ((), ())),
                preferred_element_type=jnp.float32,
            )
            s_ref[at, :] = s
            part = jnp.max(s.reshape(BLK // 8, 8, BLK), axis=0) + bias[j:j + 1, :]
            best = part if best is None else jnp.maximum(best, part)
    if qx is not None:
        sub_ref[...] = jnp.max(best, axis=0, keepdims=True) - bias
    if blend:
        return (total[0:HD] / total[HD:HD + 1]).astype(jnp.bfloat16)
    return None


MESH = pl.DeviceIdType.MESH
DIST = (1, 3, 2)
RING = [(0, 0, dz, dy) for dz in range(4) for dy in range(4) if dz or dy]
EARLY = 12


def unit_at(u):
    four, seven = (u + 12) // 16, (u + 9) // 16
    dz = (four - seven) * (u - 3) + seven * ((u + 2) // 3 - 2)
    dy = (1 - four) * u + seven * ((u + 2) % 3 + 1)
    return dz, dy


UNITS = [unit_at(u) for u in range(NB)]


def wrap(a, d):
    return lax.rem(a + d, 4)


def back(d):
    return (4 - d) % 4


def ds128(i, n=1):
    return pl.ds(pl.multiple_of(i * 128, 128), n * 128)


class Place:
    def __init__(self):
        lat, lon = lax.axis_index("lat"), lax.axis_index("lon")
        self.x, self.core, self.z, self.y = lat // 2, lax.rem(lat, 2), lon // 4, lax.rem(lon, 4)
        self.lat, self.lon = lat, lon

    def at(self, dx, dc, dz, dy):
        return (
            wrap(self.x, dx) * 2 + lax.rem(self.core + dc, 2),
            wrap(self.z, dz) * 4 + wrap(self.y, dy),
        )

    def lon_at(self, dz, dy):
        return wrap(self.z, dz) * 4 + wrap(self.y, dy)


def remote(src, dst, ss, rs, to):
    return pltpu.make_async_remote_copy(
        src_ref=src, dst_ref=dst, send_sem=ss, recv_sem=rs, device_id=to, device_id_type=MESH
    )


def arrived(buf, sem):
    pltpu.make_async_copy(buf, buf, sem).wait()


def along(half, first, second):
    return (second, first) if half == 0 else (first, second)


class Exchange:
    def __init__(self, place, piece, landing, mid, sm, rm, sf, rf):
        self.place, self.piece, self.landing, self.mid = place, piece, landing, mid
        self.sm, self.rm, self.sf, self.rf = sm, rm, sf, rf

    def start_straight(self, distances=DIST):
        place = self.place
        for n in distances:
            for d, g in ((n, 0), (0, n)):
                for half in range(2):
                    o = along(half, d, g)
                    remote(
                        self.piece(half, place.lon_at(*o)), self.landing(half, d, g, place.lon),
                        self.sf.at[half, d, g], self.rf.at[half, d, g], place.at(0, 0, *o),
                    ).start()

    def start_bent(self, d):
        place = self.place
        for g in DIST:
            for half in range(2):
                remote(
                    self.piece(half, place.lon_at(*along(half, d, g))), self.mid.at[half, d - 1, g - 1],
                    self.sm.at[half, d - 1], self.rm.at[half, d - 1], place.at(0, 0, *along(half, d, 0)),
                ).start()

    def pass_on(self, d):
        place = self.place
        for half in range(2):
            arrived(self.mid.at[half, d - 1], self.rm.at[half, d - 1])
            block = place.lon_at(*along(half, back(d), 0))
            for g in DIST:
                remote(
                    self.mid.at[half, d - 1, g - 1], self.landing(half, d, g, block),
                    self.sf.at[half, d, g], self.rf.at[half, d, g], place.at(0, 0, *along(half, 0, g)),
                ).start()

    def landed(self, half, d, g):
        block = self.place.lon_at(*along(half, back(d), back(g)))
        ref = self.landing(half, d, g, block)
        if d or g:
            arrived(ref, self.rf.at[half, d, g])
        return block, ref

    def sent(self):
        one = self.mid.at[0, 0, 0]
        for half in range(2):
            for d in range(4):
                if d:
                    arrived(self.mid.at[half, d - 1], self.sm.at[half, d - 1])
                for g in range(4):
                    if d or g:
                        arrived(one, self.sf.at[half, d, g])


def kernel(
    q, k, v, w, p, out,
    mine, kland, vland, qland, table, vt, sbuf, wbuf, sub, osend, heads, att, partial, weight, mid,
    ksm, krm, ksf, krf, vsm, vrm, vsf, vrf, qsm, qrm, qsf, qrf,
    os, orr, ws, wr, ps, pr, lsem,
):
    place = Place()
    lat, lon = place.lat, place.lon
    band_start = lat * NB
    rows = (pl.ds(0, HALF), pl.ds(HALF, HALF))
    loads = [pltpu.make_async_copy(a, mine.at[n], lsem.at[n]) for n, a in enumerate((k, v, q))]
    for c in loads:
        c.start()
    local = [
        pltpu.make_async_copy(k.at[:, ds128(lon)], kland.at[lon], lsem.at[3]),
        pltpu.make_async_copy(v.at[:, ds128(lon)], vland.at[lon], lsem.at[4]),
        pltpu.make_async_copy(q.at[:, ds128(lon)], qland.at[0], lsem.at[5]),
        pltpu.make_async_copy(w, weight.at[lat], lsem.at[6]),
        pltpu.make_async_copy(p, table.at[lon], lsem.at[7]),
    ]
    for c in local:
        c.start()

    peers = RING + [(1, 0, 0, 0), (3, 0, 0, 0), (0, 1, 0, 0)]
    bar = pltpu.get_barrier_semaphore()
    with jax.named_scope("barrier"):
        for o in peers:
            pl.semaphore_signal(bar, inc=1, device_id=place.at(*o), device_id_type=MESH)
        pl.semaphore_wait(bar, len(peers))

    started = []

    def send(*args):
        c = remote(*args)
        c.start()
        started.append(c)

    for n, o in enumerate(RING):
        send(p, table.at[lon], ps.at[n], pr.at[n], place.at(*o))

    def exchange(n, landing, *sems):
        return Exchange(
            place, lambda half, head: mine.at[n, rows[half], ds128(head)], landing, mid.at[n], *sems
        )

    ke = exchange(0, lambda half, d, g, b: kland.at[b, rows[half]], ksm, krm, ksf, krf)
    ve = exchange(1, lambda half, d, g, b: vland.at[b, rows[half]], vsm, vrm, vsf, vrf)
    qe = exchange(
        2, lambda half, d, g, b: qland.at[UNITS.index(along(half, d, g)), rows[half]], qsm, qrm, qsf, qrf
    )
    with jax.named_scope("starts"):
        for n, e in enumerate((ke, ve)):
            loads[n].wait()
            for d in DIST:
                e.start_bent(d)
            e.start_straight()
            if n == 0:
                send(w, weight.at[lat], ws.at[0], wr.at[0], place.at(1, 0, 0, 0))
                send(w, weight.at[lat], ws.at[1], wr.at[1], place.at(3, 0, 0, 0))
                send(w, weight.at[lat], ws.at[2], wr.at[2], place.at(0, 1, 0, 0))
        loads[2].wait()
    with jax.named_scope("k_pass"):
        for d in DIST:
            ke.pass_on(d)
    with jax.named_scope("v_pass"):
        for d in DIST:
            ve.pass_on(d)

    with jax.named_scope("table"):
        for c in local:
            c.wait()
        for n in range(len(RING)):
            arrived(table.at[0], pr.at[n])
        vt[HD:VR, :] = jnp.where(
            lax.broadcasted_iota(jnp.int32, (VR - HD, NB * BLK), 0) == 0, 1.0, 0.0
        ).astype(jnp.bfloat16)

    def turn(half, dz, dy):
        b, ref = ve.landed(half, *along(half, dz, dy))
        vt[0:HD, ds128(2 * b + half)] = ref[...].T

    def score_args(u):
        dz, dy = unit_at(u)
        b = place.lon_at(back(dz), back(dy))
        return split_q(qland[u]), bias_of(table[b], b, band_start)

    def turn_step(**kwargs):
        return step(sbuf, wbuf, sub, vt, kland, **kwargs)

    with jax.named_scope("turn1"):
        for half in range(2):
            for dz, dy in UNITS[:7]:
                turn(half, dz, dy)
    with jax.named_scope("k_wait"):
        for dz, dy in UNITS[1:]:
            for half in range(2):
                ke.landed(half, *along(half, dz, dy))
    with jax.named_scope("q_start"):
        qe.start_straight(DIST[:1])
        for d in DIST:
            qe.start_bent(d)
        qe.start_straight(DIST[1:])
    with jax.named_scope("score0"):
        qx, bias = score_args(0)
        turn_step(qx=qx, bias=bias, weigh=False, blend=False)
    with jax.named_scope("turn2"):
        for dz, dy in UNITS[7:]:
            for half in range(2):
                turn(half, dz, dy)

    left, right, far = (wrap(place.x, n) * 2 + place.core for n in (3, 1, 2))
    top, low = pl.ds(0, D // 2), pl.ds(D // 2, D // 2)

    def ring(src, n, to):
        send(src, src, ws.at[n], wr.at[n], to)

    def weight_near():
        arrived(weight.at[left], wr.at[0])
        ring(weight.at[left, top], 3, place.at(1, 0, 0, 0))
        ring(weight.at[left], 4, place.at(0, 1, 0, 0))
        arrived(weight.at[right], wr.at[1])
        ring(weight.at[right, low], 5, place.at(3, 0, 0, 0))
        ring(weight.at[right], 6, place.at(0, 1, 0, 0))

    def weight_far():
        arrived(weight.at[far, top], wr.at[3])
        ring(weight.at[far, top], 7, place.at(0, 1, 0, 0))
        arrived(weight.at[far, low], wr.at[5])
        ring(weight.at[far, low], 8, place.at(0, 1, 0, 0))

    def give_back(u):
        dz, dy = unit_at(u)
        remote(
            osend.at[u], heads.at[u], os.at[u], orr.at[u], place.at(0, 0, back(dz), back(dy))
        ).start()

    def wait_unit(u):
        dz, dy = unit_at(u)
        arrived(qland.at[0, rows[0]], qrf.at[0, dy, dz])
        arrived(qland.at[0, rows[1]], qrf.at[1, dz, dy])

    def body(u, _):
        with jax.named_scope("q_wait"):
            wait_unit(u + 1)
        qx, bias = score_args(u + 1)
        osend[u - 1] = turn_step(qx=qx, bias=bias)
        return 0

    def body_send(u, _):
        give_back(u - 2)
        return body(u, _)

    with jax.named_scope("w_near"):
        weight_near()
    with jax.named_scope("first_unit"):
        wait_unit(1)
        qx, bias = score_args(1)
        turn_step(qx=qx, bias=bias, blend=False)
    lax.fori_loop(1, 3, body, 0)
    with jax.named_scope("passes"):
        for d in DIST:
            qe.pass_on(d)
    lax.fori_loop(3, 12, body_send, 0)
    with jax.named_scope("w_far"):
        weight_far()
    lax.fori_loop(12, NB - 1, body_send, 0)
    with jax.named_scope("last_units"):
        give_back(NB - 3)
        osend[NB - 2] = turn_step()
        osend[NB - 1] = turn_step(weigh=False)
        give_back(NB - 2)

    with jax.named_scope("w_wait"):
        for n in (2, 4, 6):
            arrived(weight.at[0], wr.at[n])
        for n in (7, 8):
            arrived(weight.at[0, top], wr.at[n])
    give_back(NB - 1)

    def fetch(units):
        for u in units:
            if u:
                arrived(osend.at[0], orr.at[u])
        for u in units:
            att[:, u * HD:(u + 1) * HD] = (heads if u else osend)[u].T

    def weight_rows(units, n):
        return jnp.concatenate(
            [weight[n, ds128(place.lon_at(*UNITS[u])), :] for u in units], axis=0
        )

    with jax.named_scope("fetch1"):
        fetch(range(EARLY))

    def first(n, _):
        for m in (2 * n, 2 * n + 1):
            partial[m] = jnp.dot(
                att[:, 0:EARLY * HD], weight_rows(range(EARLY), m), preferred_element_type=jnp.float32
            )
        return 0

    with jax.named_scope("proj1"):
        lax.fori_loop(0, 4, first, 0)
    with jax.named_scope("fetch2"):
        fetch(range(EARLY, NB))
    with jax.named_scope("proj2"):
        for n in range(8):
            out[:, n * 256:(n + 1) * 256] = (
                partial[n]
                + jnp.dot(
                    att[:, EARLY * HD:], weight_rows(range(EARLY, NB), n),
                    preferred_element_type=jnp.float32,
                )
            ).astype(jnp.bfloat16)
    with jax.named_scope("drain"):
        for e in (ke, ve, qe):
            e.sent()
        for c in started:
            c.wait_send()
        for u in range(1, NB):
            arrived(osend.at[0], os.at[u])


def per_device(queries, keys, values, partners, out_weight):
    hbm, vmem = pl.BlockSpec(memory_space=pltpu.HBM), pl.BlockSpec(memory_space=pltpu.VMEM)
    dma = pltpu.SemaphoreType.DMA
    bf16, f32 = jnp.bfloat16, jnp.float32
    return pl.pallas_call(
        kernel,
        out_shape=jax.ShapeDtypeStruct((BLK, D), bf16),
        in_specs=[hbm] * 4 + [vmem],
        out_specs=vmem,
        scratch_shapes=[
            pltpu.VMEM((3, BLK, D), bf16),
            pltpu.VMEM((NB, BLK, HD), bf16),
            pltpu.VMEM((NB, BLK, HD), bf16),
            pltpu.VMEM((NB, BLK, HD), bf16),
            pltpu.VMEM((NB, 1, SLOTS), jnp.int32),
            pltpu.VMEM((VR, NB * BLK), bf16),
            pltpu.VMEM((NB * BLK, BLK), f32),
            pltpu.VMEM((NB * BLK, BLK), bf16),
            pltpu.VMEM((NB, BLK), f32),
            pltpu.VMEM((NB, HD, BLK), bf16),
            pltpu.VMEM((NB, HD, BLK), bf16),
            pltpu.VMEM((BLK, D), bf16),
            pltpu.VMEM((8, BLK, 256), f32),
            pltpu.VMEM((8, D, 256), bf16),
            pltpu.VMEM((3, 2, 3, 3, HALF, HD), bf16),
        ]
        + [dma((2, 3)), dma((2, 3)), dma((2, 4, 4)), dma((2, 4, 4))] * 3
        + [dma((NB,)), dma((NB,)), dma((9,)), dma((9,)), dma((15,)), dma((15,)), dma((8,))],
        name="band_attention",
        compiler_params=pltpu.CompilerParams(
            collective_id=0, has_side_effects=True, vmem_limit_bytes=VMEM_MIB * 1024 * 1024
        ),
    )(queries, keys, values, out_weight, partners)


VMEM_MIB = 40


def solution(mesh):
    return jax.shard_map(
        per_device,
        mesh=mesh,
        in_specs=(
            P(("lat", "lon"), None),
            P(("lat", "lon"), None),
            P(("lat", "lon"), None),
            P(("lat", "lon"), None),
            P(None, "lat"),
        ),
        out_specs=P(("lat", "lon"), None),
        check_vma=False,
    )
```

time: 77.9 us -> 73.5 us (0.944)
  Pallas kernels: 73.8 us -> 65.7 us
  local copies, waits for them, and re-layouts: 3.56 us -> 6.52 us
    pallas_call x1, Pallas kernels: 73.8 us -> 65.7 us  [per_device(): pl.pallas_call(kernel, out_shape=jax.ShapeDtypeStruct((BLK, D), bf16), in...]
    unnamed x3 -> x11, local copies, waits for them, and re-layouts: 2.96 us -> 6.52 us
where the time goes in v2:
time: 73.5 us; the launch traced here: 72.2 us
  Pallas kernels  65.7 us (89%)
  local copies, waits for them, and re-layouts  6.52 us (9%)
    pallas_call x1, Pallas kernels, per_device(): pl.pallas_call(kernel, out_shape=jax.ShapeDtypeStruct((BLK, D), bf16), in...  65.7 us
    unnamed x11, local copies, waits for them, and re-layouts  6.52 us

profile of v2, /device:TPU:1, one launch (start us, length us, event | category | flops | bytes accessed | tf_op | source)
XLA Modules:
  0.0 72.2 jit_solution(4415635856651307463)
XLA Ops:
  0.0 0.0 copy-start
  0.0 1.2 %copy-done = bf16[256,2048]{1,0:T(8,128)(2,1)S(1)} copy-done((bf16[256,2048]{1,0:T(8,128)(2,1)S(1)}, bf16[256,2048]{1,0:T(8,128)(2,1)}, u32[]{:S(2)}) %copy-start) | copy-done | bytes 1048600
  1.2 0.0 copy-start.1
  1.2 1.2 %copy-done.1 = bf16[256,2048]{1,0:T(8,128)(2,1)S(1)} copy-done((bf16[256,2048]{1,0:T(8,128)(2,1)S(1)}, bf16[256,2048]{1,0:T(8,128)(2,1)}, u32[]{:S(2)}) %copy-start.1) | copy-done | bytes 1048600
  2.5 0.0 copy-start.2
  2.5 1.2 %copy-done.2 = bf16[256,2048]{1,0:T(8,128)(2,1)S(1)} copy-done((bf16[256,2048]{1,0:T(8,128)(2,1)S(1)}, bf16[256,2048]{1,0:T(8,128)(2,1)}, u32[]{:S(2)}) %copy-start.2) | copy-done | bytes 1048600
  3.7 0.0 copy-start.3
  3.7 1.2 %copy-done.3 = bf16[2048,256]{1,0:T(8,128)(2,1)S(1)} copy-done((bf16[2048,256]{1,0:T(8,128)(2,1)S(1)}, bf16[2048,256]{1,0:T(8,128)(2,1)}, u32[]{:S(2)}) %copy-start.3) | copy-done | bytes 1048600
  4.9 0.0 copy-start.4
  4.9 0.7 copy-done.4
  5.6 65.7 %band_attention.1 = bf16[256,2048]{1,0:T(8,128)(2,1)S(1)} custom-call(bf16[256,2048]{1,0:T(8,128)(2,1)S(1)} %copy-done, bf16[256,2048]{1,0:T(8,128)(2,1)S(1)} %copy-done.1, bf16[256,2048]{1,0:T(8,128)(2,1)S(1)} %copy-done.2, bf16[2048,256]{1,0:T(8,128)(2,1)S(1)} %copy-done.3, s32[1,13]{1,0:T(1,128)S(1)} %copy-done.4), custom_call_target="tpu_custom_call" | custom-call | tf_op jit(solution)/shard_map/band_attention/pallas_call | solution.py:402
  71.3 1.0 %copy.7 = bf16[256,2048]{1,0:T(8,128)(2,1)} copy(bf16[256,2048]{1,0:T(8,128)(2,1)S(1)} %band_attention.1) | data formatting | bytes 2097152
Async XLA Ops:
  0.0 1.2 %copy-start = (bf16[256,2048]{1,0:T(8,128)(2,1)S(1)}, bf16[256,2048]{1,0:T(8,128)(2,1)}, u32[]{:S(2)}) copy-start(bf16[256,2048]{1,0:T(8,128)(2,1)} %q.1) | copy-start | bytes 3145732
  1.2 1.2 %copy-start.1 = (bf16[256,2048]{1,0:T(8,128)(2,1)S(1)}, bf16[256,2048]{1,0:T(8,128)(2,1)}, u32[]{:S(2)}) copy-start(bf16[256,2048]{1,0:T(8,128)(2,1)} %k.1) | copy-start | bytes 3145732
  2.5 1.2 %copy-start.2 = (bf16[256,2048]{1,0:T(8,128)(2,1)S(1)}, bf16[256,2048]{1,0:T(8,128)(2,1)}, u32[]{:S(2)}) copy-start(bf16[256,2048]{1,0:T(8,128)(2,1)} %v.1) | copy-start | bytes 3145732
  3.7 1.2 %copy-start.3 = (bf16[2048,256]{1,0:T(8,128)(2,1)S(1)}, bf16[2048,256]{1,0:T(8,128)(2,1)}, u32[]{:S(2)}) copy-start(bf16[2048,256]{1,0:T(8,128)(2,1)} %w.1) | copy-start | bytes 3145732
  4.9 0.7 copy-start.4

commit v3 on v2

--- a/solution.py
+++ b/solution.py
@@ -119,9 +119,9 @@
 
 
 class Exchange:
-    def __init__(self, place, piece, landing, mid, sm, rm, sf, rf):
+    def __init__(self, place, piece, landing, mid, final, sm, rm):
         self.place, self.piece, self.landing, self.mid = place, piece, landing, mid
-        self.sm, self.rm, self.sf, self.rf = sm, rm, sf, rf
+        self.final, self.sm, self.rm = final, sm, rm
 
     def start_straight(self, distances=DIST):
         place = self.place
@@ -131,7 +131,7 @@
                     o = along(half, d, g)
                     remote(
                         self.piece(half, place.lon_at(*o)), self.landing(half, d, g, place.lon),
-                        self.sf.at[half, d, g], self.rf.at[half, d, g], place.at(0, 0, *o),
+                        self.sm, self.final(half, d, g), place.at(0, 0, *o),
                     ).start()
 
     def start_bent(self, d):
@@ -140,7 +140,7 @@
             for half in range(2):
                 remote(
                     self.piece(half, place.lon_at(*along(half, d, g))), self.mid.at[half, d - 1, g - 1],
-                    self.sm.at[half, d - 1], self.rm.at[half, d - 1], place.at(0, 0, *along(half, d, 0)),
+                    self.sm, self.rm.at[half, d - 1], place.at(0, 0, *along(half, d, 0)),
                 ).start()
 
     def pass_on(self, d):
@@ -151,32 +151,18 @@
             for g in DIST:
                 remote(
                     self.mid.at[half, d - 1, g - 1], self.landing(half, d, g, block),
-                    self.sf.at[half, d, g], self.rf.at[half, d, g], place.at(0, 0, *along(half, 0, g)),
+                    self.sm, self.final(half, d, g), place.at(0, 0, *along(half, 0, g)),
                 ).start()
 
-    def landed(self, half, d, g):
-        block = self.place.lon_at(*along(half, back(d), back(g)))
-        ref = self.landing(half, d, g, block)
-        if d or g:
-            arrived(ref, self.rf.at[half, d, g])
-        return block, ref
-
-    def sent(self):
-        one = self.mid.at[0, 0, 0]
-        for half in range(2):
-            for d in range(4):
-                if d:
-                    arrived(self.mid.at[half, d - 1], self.sm.at[half, d - 1])
-                for g in range(4):
-                    if d or g:
-                        arrived(one, self.sf.at[half, d, g])
+    def block_at(self, half, d, g):
+        return self.place.lon_at(*along(half, back(d), back(g)))
 
 
 def kernel(
     q, k, v, w, p, out,
     mine, kland, vland, qland, table, vt, sbuf, wbuf, sub, osend, heads, att, partial, weight, mid,
-    ksm, krm, ksf, krf, vsm, vrm, vsf, vrf, qsm, qrm, qsf, qrf,
-    os, orr, ws, wr, ps, pr, lsem,
+    krm, vrm, qrm, sent, klanded, vlanded, qlanded,
+    orr, wr, ps, pr, lsem,
 ):
     place = Place()
     lat, lon = place.lat, place.lon
@@ -202,26 +188,35 @@
             pl.semaphore_signal(bar, inc=1, device_id=place.at(*o), device_id_type=MESH)
         pl.semaphore_wait(bar, len(peers))
 
-    started = []
-
-    def send(*args):
-        c = remote(*args)
+    rows_sent = [
+        remote(p, table.at[lon], ps.at[n], pr.at[n], place.at(*o)) for n, o in enumerate(RING)
+    ]
+    for c in rows_sent:
         c.start()
-        started.append(c)
-
-    for n, o in enumerate(RING):
-        send(p, table.at[lon], ps.at[n], pr.at[n], place.at(*o))
-
-    def exchange(n, landing, *sems):
+
+    def exchange(n, landing, final, rm):
         return Exchange(
-            place, lambda half, head: mine.at[n, rows[half], ds128(head)], landing, mid.at[n], *sems
+            place, lambda half, head: mine.at[n, rows[half], ds128(head)], landing, mid.at[n],
+            final, sent.at[n], rm,
         )
 
-    ke = exchange(0, lambda half, d, g, b: kland.at[b, rows[half]], ksm, krm, ksf, krf)
-    ve = exchange(1, lambda half, d, g, b: vland.at[b, rows[half]], vsm, vrm, vsf, vrf)
+    def unit_of(half, d, g):
+        return UNITS.index(along(half, d, g))
+
+    ke = exchange(
+        0, lambda half, d, g, b: kland.at[b, rows[half]], lambda half, d, g: klanded, krm
+    )
+    ve = exchange(
+        1, lambda half, d, g, b: vland.at[b, rows[half]],
+        lambda half, d, g: vlanded.at[1 if d and g else 0], vrm,
+    )
     qe = exchange(
-        2, lambda half, d, g, b: qland.at[UNITS.index(along(half, d, g)), rows[half]], qsm, qrm, qsf, qrf
+        2, lambda half, d, g, b: qland.at[unit_of(half, d, g), rows[half]],
+        lambda half, d, g: qlanded.at[unit_of(half, d, g)], qrm,
     )
+    def send_weight(src, dst, n, to):
+        remote(src, dst, sent.at[3], wr.at[n], to).start()
+
     with jax.named_scope("starts"):
         for n, e in enumerate((ke, ve)):
             loads[n].wait()
@@ -229,9 +224,9 @@
                 e.start_bent(d)
             e.start_straight()
             if n == 0:
-                send(w, weight.at[lat], ws.at[0], wr.at[0], place.at(1, 0, 0, 0))
-                send(w, weight.at[lat], ws.at[1], wr.at[1], place.at(3, 0, 0, 0))
-                send(w, weight.at[lat], ws.at[2], wr.at[2], place.at(0, 1, 0, 0))
+                send_weight(w, weight.at[lat], 0, place.at(1, 0, 0, 0))
+                send_weight(w, weight.at[lat], 1, place.at(3, 0, 0, 0))
+                send_weight(w, weight.at[lat], 2, place.at(0, 1, 0, 0))
         loads[2].wait()
     with jax.named_scope("k_pass"):
         for d in DIST:
@@ -239,6 +234,7 @@
     with jax.named_scope("v_pass"):
         for d in DIST:
             ve.pass_on(d)
+        qe.start_straight()
 
     with jax.named_scope("table"):
         for c in local:
@@ -250,8 +246,8 @@
         ).astype(jnp.bfloat16)
 
     def turn(half, dz, dy):
-        b, ref = ve.landed(half, *along(half, dz, dy))
-        vt[0:HD, ds128(2 * b + half)] = ref[...].T
+        b = place.lon_at(back(dz), back(dy))
+        vt[0:HD, ds128(2 * b + half)] = vland[b, rows[half]].T
 
     def score_args(u):
         dz, dy = unit_at(u)
@@ -261,32 +257,37 @@
     def turn_step(**kwargs):
         return step(sbuf, wbuf, sub, vt, kland, **kwargs)
 
+    def wait_unit(u):
+        arrived(qland.at[0], qlanded.at[u])
+
     with jax.named_scope("turn1"):
+        arrived(vland.at[0:6], vlanded.at[0])
         for half in range(2):
             for dz, dy in UNITS[:7]:
                 turn(half, dz, dy)
     with jax.named_scope("k_wait"):
-        for dz, dy in UNITS[1:]:
-            for half in range(2):
-                ke.landed(half, *along(half, dz, dy))
+        arrived(kland.at[0:NB - 1], klanded)
     with jax.named_scope("q_start"):
-        qe.start_straight(DIST[:1])
         for d in DIST:
             qe.start_bent(d)
-        qe.start_straight(DIST[1:])
     with jax.named_scope("score0"):
         qx, bias = score_args(0)
         turn_step(qx=qx, bias=bias, weigh=False, blend=False)
     with jax.named_scope("turn2"):
+        arrived(vland.at[0:9], vlanded.at[1])
         for dz, dy in UNITS[7:]:
             for half in range(2):
                 turn(half, dz, dy)
+    with jax.named_scope("first_unit"):
+        wait_unit(1)
+        qx, bias = score_args(1)
+        turn_step(qx=qx, bias=bias, blend=False)
 
     left, right, far = (wrap(place.x, n) * 2 + place.core for n in (3, 1, 2))
     top, low = pl.ds(0, D // 2), pl.ds(D // 2, D // 2)
 
     def ring(src, n, to):
-        send(src, src, ws.at[n], wr.at[n], to)
+        send_weight(src, src, n, to)
 
     def weight_near():
         arrived(weight.at[left], wr.at[0])
@@ -305,13 +306,8 @@
     def give_back(u):
         dz, dy = unit_at(u)
         remote(
-            osend.at[u], heads.at[u], os.at[u], orr.at[u], place.at(0, 0, back(dz), back(dy))
+            osend.at[u], heads.at[u], sent.at[4], orr.at[(u + 4) // NB], place.at(0, 0, back(dz), back(dy))
         ).start()
-
-    def wait_unit(u):
-        dz, dy = unit_at(u)
-        arrived(qland.at[0, rows[0]], qrf.at[0, dy, dz])
-        arrived(qland.at[0, rows[1]], qrf.at[1, dz, dy])
 
     def body(u, _):
         with jax.named_scope("q_wait"):
@@ -326,10 +322,6 @@
 
     with jax.named_scope("w_near"):
         weight_near()
-    with jax.named_scope("first_unit"):
-        wait_unit(1)
-        qx, bias = score_args(1)
-        turn_step(qx=qx, bias=bias, blend=False)
     lax.fori_loop(1, 3, body, 0)
     with jax.named_scope("passes"):
         for d in DIST:
@@ -352,9 +344,8 @@
     give_back(NB - 1)
 
     def fetch(units):
-        for u in units:
-            if u:
-                arrived(osend.at[0], orr.at[u])
+        late = units[0] // EARLY
+        arrived(heads.at[0:(NB - EARLY if late else EARLY - 1)], orr.at[late])
         for u in units:
             att[:, u * HD:(u + 1) * HD] = (heads if u else osend)[u].T
 
@@ -387,12 +378,12 @@
                 )
             ).astype(jnp.bfloat16)
     with jax.named_scope("drain"):
-        for e in (ke, ve, qe):
-            e.sent()
-        for c in started:
+        for n in range(3):
+            arrived(mine.at[:, 0:HALF], sent.at[n])
+        arrived(weight.at[0:7], sent.at[3])
+        arrived(osend.at[0:NB - 1], sent.at[4])
+        for c in rows_sent:
             c.wait_send()
-        for u in range(1, NB):
-            arrived(osend.at[0], os.at[u])
 
 
 def per_device(queries, keys, values, partners, out_weight):
@@ -421,8 +412,9 @@
             pltpu.VMEM((8, D, 256), bf16),
             pltpu.VMEM((3, 2, 3, 3, HALF, HD), bf16),
         ]
-        + [dma((2, 3)), dma((2, 3)), dma((2, 4, 4)), dma((2, 4, 4))] * 3
-        + [dma((NB,)), dma((NB,)), dma((9,)), dma((9,)), dma((15,)), dma((15,)), dma((8,))],
+        + [dma((2, 3))] * 3
+        + [dma((5,)), dma, dma((2,)), dma((NB,))]
+        + [dma((2,)), dma((9,)), dma((15,)), dma((15,)), dma((8,))],
         name="band_attention",
         compiler_params=pltpu.CompilerParams(
             collective_id=0, has_side_effects=True, vmem_limit_bytes=VMEM_MIB * 1024 * 1024
@@ -430,7 +422,7 @@
     )(queries, keys, values, out_weight, partners)
 
 
-VMEM_MIB = 40
+VMEM_MIB = 56
 
 
 def solution(mesh):

time: 73.5 us -> 66.3 us (0.902); the launches traced: 72.2 us -> 66.1 us
  local copies, waits for them, and re-layouts: 6.52 us -> 2.3 us
  Pallas kernels: 65.7 us -> 63.8 us
    unnamed x11 -> x1, local copies, waits for them, and re-layouts: 6.52 us -> 2.3 us
    pallas_call x1, Pallas kernels: 65.7 us -> 63.8 us  [per_device(): pl.pallas_call(kernel, out_shape=jax.ShapeDtypeStruct((BLK, D), bf16), in...]
where the time goes in v3:
time: 66.3 us; the launch traced here: 66.1 us
  Pallas kernels  63.8 us (96%)
  local copies, waits for them, and re-layouts  2.3 us (3%)
    pallas_call x1, Pallas kernels, per_device(): pl.pallas_call(kernel, out_shape=jax.ShapeDtypeStruct((BLK, D), bf16), in...  63.8 us
    unnamed x1, local copies, waits for them, and re-layouts  2.3 us

profile of v3, /device:TPU:1, one launch (start us, length us, event | category | flops | bytes accessed | tf_op | source)
XLA Modules:
  0.0 66.1 jit_solution(5231195458197168846)
XLA Ops:
  0.0 63.8 %band_attention.1 = bf16[256,2048]{1,0:T(8,128)(2,1)} custom-call(bf16[256,2048]{1,0:T(8,128)(2,1)} %q.1, bf16[256,2048]{1,0:T(8,128)(2,1)} %k.1, bf16[256,2048]{1,0:T(8,128)(2,1)} %v.1, bf16[2048,256]{1,0:T(8,128)(2,1)} %w.1, s32[1,13]{1,0:T(1,128)} %p.1), custom_call_target="tpu_custom_call" | custom-call | tf_op jit(solution)/shard_map/band_attention/pallas_call | solution.py:393
  63.8 2.3 %copy.7 = bf16[256,2048]{1,0:T(8,128)(2,1)} copy(bf16[256,2048]{1,0:T(8,128)(2,1)} %band_attention.1) | data formatting | bytes 2097152

commit v4 on v3

--- a/solution.py
+++ b/solution.py
@@ -159,8 +159,8 @@
 
 
 def kernel(
-    q, k, v, w, p, out,
-    mine, kland, vland, qland, table, vt, sbuf, wbuf, sub, osend, heads, att, partial, weight, mid,
+    q, k, v, w, p, result,
+    out, osem, mine, kland, vland, qland, table, vt, sbuf, wbuf, sub, osend, heads, att, partial, weight, mid,
     krm, vrm, qrm, sent, klanded, vlanded, qlanded,
     orr, wr, ps, pr, lsem,
 ):
@@ -368,6 +368,10 @@
         lax.fori_loop(0, 4, first, 0)
     with jax.named_scope("fetch2"):
         fetch(range(EARLY, NB))
+    def put(n):
+        tile = pl.ds(n * 256, 256)
+        return pltpu.make_async_copy(out.at[:, tile], result.at[:, tile], osem.at[n])
+
     with jax.named_scope("proj2"):
         for n in range(8):
             out[:, n * 256:(n + 1) * 256] = (
@@ -377,7 +381,10 @@
                     preferred_element_type=jnp.float32,
                 )
             ).astype(jnp.bfloat16)
+            put(n).start()
     with jax.named_scope("drain"):
+        for n in range(8):
+            put(n).wait()
         for n in range(3):
             arrived(mine.at[:, 0:HALF], sent.at[n])
         arrived(weight.at[0:7], sent.at[3])
@@ -394,8 +401,10 @@
         kernel,
         out_shape=jax.ShapeDtypeStruct((BLK, D), bf16),
         in_specs=[hbm] * 4 + [vmem],
-        out_specs=vmem,
+        out_specs=hbm,
         scratch_shapes=[
+            pltpu.VMEM((BLK, D), bf16),
+            dma((8,)),
             pltpu.VMEM((3, BLK, D), bf16),
             pltpu.VMEM((NB, BLK, HD), bf16),
             pltpu.VMEM((NB, BLK, HD), bf16),

time: 66.3 us -> 66.2 us (level)
  no operation moved by 1% of the time
where the time goes in v4:
time: 66.2 us; the launch traced here: 66 us
  Pallas kernels  63.7 us (96%)
  local copies, waits for them, and re-layouts  2.3 us (3%)
    pallas_call x1, Pallas kernels, per_device(): pl.pallas_call(kernel, out_shape=jax.ShapeDtypeStruct((BLK, D), bf16), in...  63.7 us
    unnamed x1, local copies, waits for them, and re-layouts  2.3 us

profile of v4, /device:TPU:1, one launch (start us, length us, event | category | flops | bytes accessed | tf_op | source)
XLA Modules:
  0.0 66.0 jit_solution(12605633204287699806)
XLA Ops:
  0.0 63.7 %band_attention.1 = bf16[256,2048]{1,0:T(8,128)(2,1)} custom-call(bf16[256,2048]{1,0:T(8,128)(2,1)} %q.1, bf16[256,2048]{1,0:T(8,128)(2,1)} %k.1, bf16[256,2048]{1,0:T(8,128)(2,1)} %v.1, bf16[2048,256]{1,0:T(8,128)(2,1)} %w.1, s32[1,13]{1,0:T(1,128)} %p.1), custom_call_target="tpu_custom_call" | custom-call | tf_op jit(solution)/shard_map/band_attention/pallas_call | solution.py:400
  63.7 2.3 %copy.7 = bf16[256,2048]{1,0:T(8,128)(2,1)} copy(bf16[256,2048]{1,0:T(8,128)(2,1)} %band_attention.1) | data formatting | bytes 2097152
